TPU v7x, 32 devices: a whole 2x2x4 slice. The times are simulated.
32 devices in a mesh: py: 4 (over z), pz: 8 (over y, x, core).
Axes of the slice: x: 2, y: 2, z: 4, core: 2. Of those that a mesh axis runs over, the one named last changes fastest.
Arguments:
- field: bfloat16 [128, 128, 64, 256], P('py', 'pz'), may hold values from -60 to 60
- spectral_weights: bfloat16 [32, 32, 32, 2, 64, 64], P('py', 'pz'), may hold values from -0.5 to 0.5
- bypass_weight: bfloat16 [64, 64], replicated, may hold values from -0.75 to 0.75
Outputs:
- normalized: bfloat16 [128, 128, 64, 256], P('py', 'pz')
All inputs are finite; a program needn't handle non-finite values.
Results may differ from a plain program's by a relative error of at most 0.0081.
Values may be sent and summed in bfloat16 or wider, within the bound.
A program may use at most 192 MiB of HBM per device.

v0:
```python
import math

import jax
import jax.numpy as jnp
from jax import lax
from jax.sharding import PartitionSpec as P

NX = 256
NY = 128
NZ = 128
C = 64
MODES = 32


def mode_frequencies(mode_count):
    ordinal = jnp.arange(mode_count, dtype=jnp.float32)
    return jnp.where(ordinal < mode_count // 2, ordinal, ordinal - mode_count)


def phase_angles(length, mode_count):
    points = jnp.arange(length, dtype=jnp.float32)
    return 2.0 * math.pi / length * points[:, None] * mode_frequencies(mode_count)[None, :]


def real_forward(length, mode_count):
    angles = phase_angles(length, mode_count)
    matrix = jnp.stack([jnp.cos(angles), -jnp.sin(angles)], axis=2).reshape(length, 2 * mode_count)
    return (matrix / math.sqrt(length)).astype(jnp.bfloat16)


def complex_forward(length, mode_count):
    angles = phase_angles(length, mode_count)
    cosine = jnp.cos(angles)
    sine_part = jnp.sin(angles)
    from_real = jnp.stack([cosine, -sine_part], axis=2)
    from_imag = jnp.stack([sine_part, cosine], axis=2)
    return (jnp.stack([from_real, from_imag], axis=1) / math.sqrt(length)).astype(jnp.bfloat16)


def complex_inverse(length, mode_count):
    angles = phase_angles(length, mode_count).T
    cosine = jnp.cos(angles)
    sine_part = jnp.sin(angles)
    from_real = jnp.stack([cosine, sine_part], axis=2)
    from_imag = jnp.stack([-sine_part, cosine], axis=2)
    return (jnp.stack([from_real, from_imag], axis=1) / math.sqrt(mode_count)).astype(jnp.bfloat16)


def real_inverse(length, mode_count):
    angles = phase_angles(length, mode_count).T
    matrix = jnp.stack([jnp.cos(angles), -jnp.sin(angles)], axis=1).reshape(2 * mode_count, length)
    return (matrix / math.sqrt(mode_count)).astype(jnp.bfloat16)


def mix_modes(spectrum, weights):
    real_in = spectrum[..., 0]
    imag_in = spectrum[..., 1]
    real_w = weights[:, :, :, 0]
    imag_w = weights[:, :, :, 1]

    def product(operand, coefficient):
        return jnp.einsum(
            "cabk,abkco->oabk", operand, coefficient, preferred_element_type=jnp.float32
        )

    real_out = product(real_in, real_w) - product(imag_in, imag_w)
    imag_out = product(real_in, imag_w) + product(imag_in, real_w)
    return jnp.stack([real_out, imag_out], axis=-1).astype(jnp.bfloat16)


def on_device(field, spectral_weights, bypass_weight):
    row_table = real_forward(NX, MODES)
    forward_plane = complex_forward(NY, MODES)
    forward_column = complex_forward(NZ, MODES)
    inverse_column = complex_inverse(NZ, MODES)
    inverse_plane = complex_inverse(NY, MODES)
    inverse_row = real_inverse(NX, MODES)
    flat = jnp.dot(field.reshape(-1, NX), row_table, preferred_element_type=jnp.float32)
    row_modes = flat.reshape(field.shape[:3] + (2 * MODES,)).astype(jnp.bfloat16)
    incoming = lax.all_to_all(row_modes, "py", split_axis=3, concat_axis=0, tiled=True)
    paired = incoming.reshape(incoming.shape[:3] + (-1, 2))
    plane_modes = jnp.einsum(
        "yzcmp,ypkq->zcmkq", paired, forward_plane, preferred_element_type=jnp.float32
    ).astype(jnp.bfloat16)
    plane_modes = plane_modes.reshape(plane_modes.shape[:3] + (-1,))
    incoming = lax.all_to_all(plane_modes, "pz", split_axis=3, concat_axis=0, tiled=True)
    paired = incoming.reshape(incoming.shape[:3] + (-1, 2))
    spectrum = jnp.einsum(
        "zcakp,zpjq->cakjq", paired, forward_column, preferred_element_type=jnp.float32
    ).astype(jnp.bfloat16)
    mixed_modes = mix_modes(spectrum, spectral_weights)
    column_back = jnp.einsum(
        "oabkp,kpzq->zoabq", mixed_modes, inverse_column, preferred_element_type=jnp.float32
    ).astype(jnp.bfloat16)
    column_back = column_back.reshape(column_back.shape[:3] + (-1,))
    incoming = lax.all_to_all(column_back, "pz", split_axis=0, concat_axis=3, tiled=True)
    paired = incoming.reshape(incoming.shape[:3] + (-1, 2))
    plane_back = jnp.einsum(
        "zcakp,kpyq->yzcaq", paired, inverse_plane, preferred_element_type=jnp.float32
    ).astype(jnp.bfloat16)
    plane_back = plane_back.reshape(plane_back.shape[:3] + (-1,))
    incoming = lax.all_to_all(plane_back, "py", split_axis=0, concat_axis=3, tiled=True)
    points = jnp.dot(
        incoming.reshape(-1, 2 * MODES), inverse_row, preferred_element_type=jnp.float32
    )
    spectral = points.reshape(incoming.shape[:3] + (NX,))
    bypass = jnp.einsum("yzcx,co->yzox", field, bypass_weight, preferred_element_type=jnp.float32)
    activated = jax.nn.gelu(spectral + bypass, approximate=True)
    entries = NX * NY * NZ * C
    summed, squared = lax.psum((jnp.sum(activated), jnp.sum(activated * activated)), ("py", "pz"))
    field_mean = summed / entries
    field_var = squared / entries - field_mean * field_mean
    return ((activated - field_mean) * lax.rsqrt(field_var + 1e-05)).astype(jnp.bfloat16)


def solution(mesh):
    in_specs = (P("py", "pz", None, None), P("py", "pz", None, None, None, None), P())
    out_specs = P("py", "pz", None, None)
    return jax.shard_map(
        on_device, mesh=mesh, in_specs=in_specs, out_specs=out_specs, check_vma=False
    )
```

profile of v0, /device:TPU:12, one launch (start us, length us, event | category | flops | bytes accessed | tf_op | source)
XLA Modules:
  0.0 524.4 jit_solution(14442338689824171746)
XLA Ops:
  0.3 12.8 %fusion = bf16[32768,64]{0,1:T(8,128)(2,1)} fusion(bf16[256,64]{0,1:T(8,128)(2,1)S(1)} %convert_element_type.65, bf16[32768,256]{1,0:T(8,128)(2,1)} %bitcast.144), kind=kOutput, calls=%fused_computation.2 | convolution fusion | flops 1075838976 | bytes 21004288 | tf_op jit(solution)/shard_map/dot_general | solution.py:78
  13.2 11.3 %convert_element_type.68 = bf16[32,16,64,64]{2,1,0,3:T(8,128)(2,1)} reshape(bf16[32768,64]{0,1:T(8,128)(2,1)} %fusion) | data formatting | bytes 8388608 | tf_op jit(solution)/shard_map/convert_element_type | solution.py:79
  24.5 9.5 %reshape.532 = bf16[4,2,262144]{2,1,0:T(2,128)(2,1)} reshape(bf16[64,32,16,64]{3,2,1,0:T(8,128)(2,1)} %bitcast.145) | data formatting | bytes 8388608
  34.0 5.8 %all-to-all-start = ((bf16[4,2,262144]{2,1,0:T(2,128)(2,1)}), bf16[4,2,262144]{2,1,0:T(2,128)(2,1)}, u32[]{:S(2)}, u32[]{:S(2)}) async-start(bf16[4,2,262144]{2,1,0:T(2,128)(2,1)} %reshape.532), calls=%async_computation | async-start | bytes 8388608 | tf_op jit(solution)/shard_map/all_to_all | solution.py:80
  40.0 89.9 %all-to-all-done = bf16[4,2,262144]{2,1,0:T(2,128)(2,1)} async-done(((bf16[4,2,262144]{2,1,0:T(2,128)(2,1)}), bf16[4,2,262144]{2,1,0:T(2,128)(2,1)}, u32[]{:S(2)}, u32[]{:S(2)}) %all-to-all-start) | async-done | bytes 4194336 | tf_op jit(solution)/shard_map/all_to_all | solution.py:80
  129.9 9.3 %reshape.533 = bf16[64,32,16,64]{3,2,1,0:T(8,128)(2,1)} reshape(bf16[4,2,262144]{2,1,0:T(2,128)(2,1)} %all-to-all-done) | data formatting | bytes 8388608
  139.1 9.0 %copy.102 = bf16[4,32,16,64,16]{3,2,4,1,0:T(8,128)(2,1)} copy(bf16[4,32,16,64,16]{3,2,1,4,0:T(8,128)(2,1)} %bitcast.147) | data formatting | bytes 8388608 | tf_op jit(solution)/shard_map/all_to_all | solution.py:80
  148.2 13.8 %copy.120 = bf16[128,16,64,8,2,1]{0,3,4,5,2,1:T(8,128)(2,1)} copy(bf16[128,16,64,8,2,1]{2,1,4,3,0,5:T(8,128)(2,1)} %bitcast.148) | data formatting | bytes 8388608 | tf_op jit(solution)/shard_map/reshape | solution.py:81
  161.9 5.4 %bitcast_convert_fusion.1 = bf16[16,64,8,32,2]{3,2,4,1,0:T(8,128)(2,1)} fusion(bf16[128,16,64,8,2,1]{0,3,4,5,2,1:T(8,128)(2,1)} %copy.120, f32[128,1,32,2]{0,2,1,3:T(8,128)S(1)} %get-tuple-element.14, f32[128,1,32,2]{0,2,1,3:T(8,128)S(1)} %get-tuple-element.13), kind=kOutput, calls=%fused_computation.26 | convolution fusion | flops 269008896 | bytes 5308416 | tf_op jit(solution)/shard_map/yzcmp,ypkq->zcmkq/dot_general | solution.py:82
  167.3 6.0 %copy.140 = bf16[16,64,8,32,2]{1,2,0,4,3:T(8,128)(2,1)S(1)} copy(bf16[16,64,8,32,2]{3,2,4,1,0:T(8,128)(2,1)} %bitcast_convert_fusion.1) | data formatting | bytes 2097152 | tf_op jit(solution)/shard_map/reshape | solution.py:85
  173.4 2.7 reshape.534
  176.0 4.4 all-to-all-start.1
  180.6 13.7 %all-to-all-done.1 = bf16[8,2,32768]{2,1,0:T(2,128)(2,1)S(1)} async-done(((bf16[8,2,32768]{2,1,0:T(2,128)(2,1)}), bf16[8,2,32768]{2,1,0:T(2,128)(2,1)S(1)}, u32[]{:S(2)}, u32[]{:S(2)}) %all-to-all-start.1) | async-done | bytes 1048608 | tf_op jit(solution)/shard_map/all_to_all | solution.py:86
  197.7 4.5 copy.123
  203.5 8.1 %fusion.8 = f32[8,4,32,1,64]{4,3,2,1,0:T(1,128)S(1)} fusion(bf16[64,8,4,32,1]{0,4,3,2,1:T(2,128)(2,1)S(1)} %copy.125, bf16[8,4,32,2,64,64]{5,4,3,2,1,0:T(8,128)(2,1)} %param.4), kind=kOutput, calls=%fused_computation.13 | convolution fusion | flops 8388608 | bytes 17170432 | tf_op jit(solution)/shard_map/cabk,abkco->oabk/dot_general | solution.py:62
  211.6 8.1 %fusion.14 = f32[8,4,32,1,64]{4,3,2,1,0:T(1,128)S(1)} fusion(bf16[64,8,4,32,1]{0,4,3,2,1:T(2,128)(2,1)S(1)} %copy.125, bf16[8,4,32,2,64,64]{5,4,3,2,1,0:T(8,128)(2,1)} %param.4), kind=kOutput, calls=%fused_computation.19 | convolution fusion | flops 8388608 | bytes 17170432 | tf_op jit(solution)/shard_map/cabk,abkco->oabk/dot_general | solution.py:62
  220.4 8.1 %fusion.12 = f32[8,4,32,1,64]{4,3,2,1,0:T(1,128)S(1)} fusion(bf16[64,8,4,32,1]{0,4,3,2,1:T(2,128)(2,1)S(1)} %copy.127, bf16[8,4,32,2,64,64]{5,4,3,2,1,0:T(8,128)(2,1)} %param.4), kind=kOutput, calls=%fused_computation.17 | convolution fusion | flops 8388608 | bytes 17170432 | tf_op jit(solution)/shard_map/cabk,abkco->oabk/dot_general | solution.py:62
  228.5 8.3 %fusion.10 = f32[8,4,32,1,64]{4,3,2,1,0:T(1,128)S(1)} fusion(bf16[64,8,4,32,1]{0,4,3,2,1:T(2,128)(2,1)S(1)} %copy.127, bf16[8,4,32,2,64,64]{5,4,3,2,1,0:T(8,128)(2,1)} %param.4), kind=kOutput, calls=%fused_computation.15 | convolution fusion | flops 8388608 | bytes 17170432 | tf_op jit(solution)/shard_map/cabk,abkco->oabk/dot_general | solution.py:62
  238.2 3.5 copy.111
  243.4 18.4 %all_to_all.60 = bf16[8,2,32768]{2,1,0:T(2,128)(2,1)} all-to-all(bf16[8,2,32768]{2,1,0:T(2,128)(2,1)S(1)} %reshape.536), channel_id=1, replica_groups=mesh['py'=4,'pz'=8] {'pz'}, dimensions={0} | all-to-all | bytes 2097152 | tf_op jit(solution)/shard_map/all_to_all | solution.py:96
  261.8 3.1 reshape.537
  266.9 2.9 copy.114
  269.8 12.8 %copy.115 = bf16[128,16,64,16]{2,3,1,0:T(8,128)(2,1)} copy(bf16[128,16,64,16]{0,2,3,1:T(8,128)(2,1)} %bitcast.150) | data formatting | bytes 8388608 | tf_op jit(solution)/shard_map/reshape | solution.py:101
  282.6 9.5 %reshape.538 = bf16[4,2,262144]{2,1,0:T(2,128)(2,1)} reshape(bf16[128,16,16,64]{3,2,1,0:T(8,128)(2,1)} %bitcast.146) | data formatting | bytes 8388608
  292.2 8.4 %all-to-all-start.3 = ((bf16[4,2,262144]{2,1,0:T(2,128)(2,1)}), bf16[4,2,262144]{2,1,0:T(2,128)(2,1)}, u32[]{:S(2)}, u32[]{:S(2)}) async-start(bf16[4,2,262144]{2,1,0:T(2,128)(2,1)} %reshape.538), calls=%async_computation.3 | async-start | bytes 8388608 | tf_op jit(solution)/shard_map/all_to_all | solution.py:102
  300.9 89.3 %all-to-all-done.3 = bf16[4,2,262144]{2,1,0:T(2,128)(2,1)} async-done(((bf16[4,2,262144]{2,1,0:T(2,128)(2,1)}), bf16[4,2,262144]{2,1,0:T(2,128)(2,1)}, u32[]{:S(2)}, u32[]{:S(2)}) %all-to-all-start.3) | async-done | bytes 4194336 | tf_op jit(solution)/shard_map/all_to_all | solution.py:102
  390.2 9.3 %reshape.539 = bf16[128,16,16,64]{3,2,1,0:T(8,128)(2,1)} reshape(bf16[4,2,262144]{2,1,0:T(2,128)(2,1)} %all-to-all-done.3) | data formatting | bytes 8388608
  399.4 9.0 %copy.116 = bf16[32,16,64,4,16]{2,4,3,1,0:T(8,128)(2,1)} copy(bf16[32,16,64,4,16]{2,4,1,0,3:T(8,128)(2,1)} %bitcast.149) | data formatting | bytes 8388608 | tf_op jit(solution)/shard_map/all_to_all | solution.py:102
  408.5 19.0 %fusion.36 = f32[32,16,64,256]{3,2,1,0:T(8,128)} fusion(bf16[32,16,64,64]{2,3,1,0:T(8,128)(2,1)} %bitcast.143, bf16[64,256,1,1]{1,0,2,3:T(8,128)(2,1)S(1)} %reshape.529), kind=kOutput, calls=%fused_computation.62 | convolution fusion | flops 1073741824 | bytes 37781504 | tf_op jit(solution)/shard_map/dot_general | solution.py:103
  427.5 32.3 %fusion.54 = (f32[]{:T(128)}, f32[]{:T(128)}, f32[32,16,64,256]{3,2,1,0:T(8,128)}) fusion(f32[32,16,64,256]{3,2,1,0:T(8,128)} %fusion.36, bf16[32,16,64,256]{3,2,1,0:T(8,128)(2,1)} %param.3, bf16[64,64]{1,0:T(8,128)(2,1)S(1)} %copy-done), kind=kOutput, calls=%fused_computation.83 | convolution fusion | flops 1174405120 | bytes 83894280 | tf_op jit(solution)/shard_map/yzcx,co->yzox/dot_general | solution.py:107
  459.8 43.2 %all-reduce = (f32[]{:T(128)}, f32[]{:T(128)}) all-reduce(f32[]{:T(128)} %get-tuple-element.6, f32[]{:T(128)} %get-tuple-element.5), channel_id=1, replica_groups=mesh['py'=4,'pz'=8] {'py','pz'}, use_global_device_ids=true, to_apply=%region_3.4 | all-reduce | flops 2 | bytes 16 | tf_op jit(solution)/shard_map/psum | solution.py:110
  505.5 18.5 %multiply_convert_fusion = bf16[32,16,64,256]{3,2,1,0:T(8,128)(2,1)} fusion(f32[32,16,64,256]{3,2,1,0:T(8,128)} %get-tuple-element.25, f32[]{:T(128)S(6)} %rsqrt.3, f32[]{:T(128)S(6)} %div.32), kind=kLoop, calls=%fused_computation.11 | loop fusion | flops 25165824 | bytes 50331656 | tf_op jit(solution)/shard_map/convert_element_type | solution.py:113
  (29 shorter events, 11.2 us)
Async XLA Ops:
  0.0 427.5 %copy-start = (bf16[64,64]{1,0:T(8,128)(2,1)S(1)}, bf16[64,64]{1,0:T(8,128)(2,1)}, u32[]{:S(2)}) copy-start(bf16[64,64]{1,0:T(8,128)(2,1)} %param.5) | copy-start | bytes 24580
  34.0 95.8 %all-to-all-start = ((bf16[4,2,262144]{2,1,0:T(2,128)(2,1)}), bf16[4,2,262144]{2,1,0:T(2,128)(2,1)}, u32[]{:S(2)}, u32[]{:S(2)}) async-start(bf16[4,2,262144]{2,1,0:T(2,128)(2,1)} %reshape.532), calls=%async_computation | async-start | bytes 8388608 | tf_op jit(solution)/shard_map/all_to_all | solution.py:80
  176.0 18.3 %all-to-all-start.1 = ((bf16[8,2,32768]{2,1,0:T(2,128)(2,1)}), bf16[8,2,32768]{2,1,0:T(2,128)(2,1)S(1)}, u32[]{:S(2)}, u32[]{:S(2)}) async-start(bf16[8,2,32768]{2,1,0:T(2,128)(2,1)} %reshape.534), calls=%async_computation.1 | async-start | bytes 2097152 | tf_op jit(solution)/shard_map/all_to_all | solution.py:86
  292.2 98.0 %all-to-all-start.3 = ((bf16[4,2,262144]{2,1,0:T(2,128)(2,1)}), bf16[4,2,262144]{2,1,0:T(2,128)(2,1)}, u32[]{:S(2)}, u32[]{:S(2)}) async-start(bf16[4,2,262144]{2,1,0:T(2,128)(2,1)} %reshape.538), calls=%async_computation.3 | async-start | bytes 8388608 | tf_op jit(solution)/shard_map/all_to_all | solution.py:102
where the time goes:
time: 530 us; the launch traced here: 524 us
  waiting for transfers between devices  193 us (36%)
  local copies, waits for them, and re-layouts  124 us (23%)
  matrix products  104 us (20%)
  blocking collectives  61.6 us (12%)
  other arithmetic  19.5 us (4%)
  starting transfers between devices  18.7 us (4%)
    all_to_all x1, waiting for transfers between devices, on_device(): lax.all_to_all(row_modes, 'py', split_axis=3, concat_axis=0, tiled=True)  89.9 us
    all_to_all x1, waiting for transfers between devices, on_device(): lax.all_to_all(plane_back, 'py', split_axis=0, concat_axis=3, tiled=True)  89.3 us
    unnamed x10, local copies, waits for them, and re-layouts  46.5 us
    psum x1, blocking collectives, on_device(): lax.psum((jnp.sum(activated), jnp.sum(activated * activated)), ('py', 'pz'))  43.2 us
    dot_general x4, matrix products, product(): jnp.einsum('cabk,abkco->oabk', operand, coefficient, preferred_element_ty...  32.6 us
    dot_general x1, matrix products, on_device(): jnp.einsum('yzcx,co->yzox', field, bypass_weight, preferred_element_type=...  32.3 us
    dot_general x1, matrix products, on_device(): jnp.dot(incoming.reshape(-1, 2 * MODES), inverse_row, preferred_element_t...  19 us
    convert_element_type x1, other arithmetic, on_device(): ((activated - field_mean) * lax.rsqrt(field_var + 1e-05)).astype(jnp.bflo...  18.5 us
  transfers between devices with their start and end apart: 3, of which 3 were waited for; matrix products, arithmetic and copies ran while one was open for 0% of the time, Pallas kernels for 0%

commit v1 on v0

--- a/solution.py
+++ b/solution.py
@@ -1,8 +1,12 @@
+import functools
 import math
 
 import jax
 import jax.numpy as jnp
+import numpy as np
 from jax import lax
+from jax.experimental import pallas as pl
+from jax.experimental.pallas import tpu as pltpu
 from jax.sharding import PartitionSpec as P
 
 NX = 256
@@ -68,7 +72,7 @@
     return jnp.stack([real_out, imag_out], axis=-1).astype(jnp.bfloat16)
 
 
-def on_device(field, spectral_weights, bypass_weight):
+def plain_layer(field, spectral_weights, bypass_weight):
     row_table = real_forward(NX, MODES)
     forward_plane = complex_forward(NY, MODES)
     forward_column = complex_forward(NZ, MODES)
@@ -113,9 +117,435 @@
     return ((activated - field_mean) * lax.rsqrt(field_var + 1e-05)).astype(jnp.bfloat16)
 
 
+def np_angles(length, mode_count):
+    ordinal = np.arange(mode_count, dtype=np.float32)
+    frequency = np.where(ordinal < mode_count // 2, ordinal, ordinal - mode_count).astype(np.float32)
+    points = np.arange(length, dtype=np.float32)
+    scale = np.float32(2.0 * math.pi / length)
+    return scale * points[:, None] * frequency[None, :]
+
+
+def np_tables(ny, nz, nx, modes):
+    angles = np_angles(nx, modes)
+    row = np.stack([np.cos(angles), -np.sin(angles)], axis=2).reshape(nx, 2 * modes)
+    row = (row / np.float32(math.sqrt(nx))).T
+    inverse_row = np.stack([np.cos(angles.T), -np.sin(angles.T)], axis=1).reshape(2 * modes, nx)
+    inverse_row = inverse_row / np.float32(math.sqrt(modes))
+
+    def forward(length):
+        a = np_angles(length, modes)
+        c, s = np.cos(a), np.sin(a)
+        table = np.stack([np.stack([c, -s], axis=2), np.stack([s, c], axis=2)], axis=1)
+        return table / np.float32(math.sqrt(length))
+
+    def inverse(length):
+        a = np_angles(length, modes).T
+        c, s = np.cos(a), np.sin(a)
+        table = np.stack([np.stack([c, s], axis=2), np.stack([-s, c], axis=2)], axis=1)
+        return table / np.float32(math.sqrt(modes))
+
+    column = forward(nz).transpose(2, 3, 1, 0).reshape(2 * modes, 2 * nz)
+    plane = forward(ny).reshape(ny // 2, 2, 2, modes, 2).transpose(1, 3, 4, 2, 0)
+    plane = plane.reshape(4 * modes, ny)
+    back_plane = inverse(ny).reshape(modes, 2, ny // 2, 2, 2).transpose(4, 2, 3, 0, 1)
+    back_plane = back_plane.reshape(ny, 4 * modes)
+    back_column = inverse(nz).transpose(3, 2, 0, 1).reshape(2 * nz, 2 * modes)
+    tables = (row, column, plane, back_plane, back_column, inverse_row)
+    return tuple(np.asarray(t, np.float32).astype(jnp.bfloat16) for t in tables)
+
+
+MESH_ID = pl.DeviceIdType.MESH
+
+
+def greet(axis, size, me):
+    barrier = pltpu.get_barrier_semaphore()
+    for step in range(1, size):
+        pl.semaphore_signal(
+            barrier, inc=1, device_id={axis: lax.rem(me + step, size)}, device_id_type=MESH_ID
+        )
+    pl.semaphore_wait(barrier, size - 1)
+
+
+def send_pieces(axis, size, me, source_of, target, send_sem, recv_sem):
+    for step in range(1, size):
+        peer = lax.rem(me + step, size)
+        pltpu.make_async_remote_copy(
+            src_ref=source_of(peer),
+            dst_ref=target,
+            send_sem=send_sem.at[step],
+            recv_sem=recv_sem.at[step],
+            device_id={axis: peer},
+            device_id_type=MESH_ID,
+        ).start()
+    pltpu.make_async_copy(source_of(me), target, send_sem.at[0]).start()
+
+
+def wait_pieces(size, me, source_of, place_of, send_sem, recv_sem):
+    for step in range(1, size):
+        sent = source_of(lax.rem(me + step, size))
+        pltpu.make_async_copy(sent, sent, send_sem.at[step]).wait()
+        place = place_of(lax.rem(me + size - step, size))
+        pltpu.make_async_copy(place, place, recv_sem.at[step]).wait()
+    own = source_of(me)
+    pltpu.make_async_copy(own, own, send_sem.at[0]).wait()
+
+
+def dot(a, b):
+    return jnp.dot(a, b, preferred_element_type=jnp.float32)
+
+
+NT = (((1,), (1,)), ((), ()))
+TN = (((0,), (0,)), ((), ()))
+
+
+def row_kernel(size, steps, field_ref, table_ref, out_ref, held, wide, send_sem, recv_sem):
+    step = pl.program_id(0)
+    me = lax.axis_index("pz")
+    rows, zs, cs, nx = field_ref.shape
+    modes2 = table_ref.shape[0]
+    group = modes2 // size
+
+    @pl.when(step == 0)
+    def _():
+        greet("pz", size, me)
+
+    for z in range(zs):
+        block = field_ref[:, z].reshape(rows * cs, nx)
+        wide[pl.ds(z, modes2, stride=zs), :] = lax.dot_general(
+            table_ref[...], block, NT, preferred_element_type=jnp.float32
+        )
+    held[step] = wide[...].astype(jnp.bfloat16).reshape(modes2, zs, rows * cs)
+
+    send_pieces(
+        "pz", size, me,
+        lambda peer: held.at[step, pl.ds(peer * group, group)],
+        out_ref.at[step, :, pl.ds(pl.multiple_of(me * zs, zs), zs)],
+        send_sem, recv_sem,
+    )
+
+    @pl.when(step == steps - 1)
+    def _():
+        wait_pieces(
+            size, me,
+            lambda peer: held.at[:, pl.ds(peer * group, group)],
+            lambda peer: out_ref.at[:, :, pl.ds(pl.multiple_of(peer * zs, zs), zs)],
+            send_sem, recv_sem,
+        )
+
+
+def column_kernel(size, steps, in_ref, table_ref, out_ref, held, wide, send_sem, recv_sem):
+    step = pl.program_id(0)
+    me = lax.axis_index("py")
+    modes2 = table_ref.shape[0]
+    kxs, _, _, lanes = held.shape
+    nz = in_ref.shape[2]
+    group = modes2 // size
+
+    @pl.when(step == 0)
+    def _():
+        greet("py", size, me)
+
+    for kx in range(kxs):
+        rhs = in_ref[0, 2 * kx : 2 * kx + 2].reshape(2 * nz, lanes)
+        wide[pl.ds(kx * modes2 * steps + step, modes2, stride=steps), :] = dot(table_ref[...], rhs)
+
+    @pl.when(step == steps - 1)
+    def _():
+        for kx in range(kxs):
+            part = wide[kx * modes2 * steps : (kx + 1) * modes2 * steps, :]
+            held[kx] = part.astype(jnp.bfloat16).reshape(modes2, steps, lanes)
+        source_of = lambda peer: held.at[:, pl.ds(peer * group, group)]
+        place_of = lambda peer: out_ref.at[:, :, pl.ds(pl.multiple_of(peer * steps, steps), steps)]
+        send_pieces("py", size, me, source_of, place_of(me), send_sem, recv_sem)
+        wait_pieces(size, me, source_of, place_of, send_sem, recv_sem)
+
+
+def plane_kernel(in_ref, table_ref, out_ref):
+    _, kzs2, ys, lanes = in_ref.shape
+    half = lanes // 2
+    modes2 = table_ref.shape[0] // 2
+    for kz in range(kzs2 // 2):
+        rhs = in_ref[0, 2 * kz : 2 * kz + 2].reshape(2 * ys, lanes)
+        both = dot(table_ref[...], rhs)
+        out_ref[0, kz] = (both[:modes2, :half] + both[modes2:, half:]).astype(jnp.bfloat16)
+
+
+def back_plane_kernel(size, in_ref, table_ref, out_ref, held, wide, send_sem, recv_sem):
+    me = lax.axis_index("py")
+    kxs, kzs, modes2, cs = in_ref.shape
+    _, _, steps, group, lanes = held.shape
+    half = size * steps
+    greet("py", size, me)
+    zero = jnp.zeros((modes2, cs), jnp.bfloat16)
+    for kx in range(kxs):
+        for kz in range(kzs):
+            piece = in_ref[kx, kz]
+            rhs = jnp.concatenate(
+                [jnp.concatenate([piece, zero], 1), jnp.concatenate([zero, piece], 1)], 0
+            )
+            val = dot(table_ref[...], rhs)
+            for q in range(2):
+                for peer in range(size):
+                    start = q * half + peer * steps
+                    first = (peer * kxs + kx) * steps * group + 2 * kz + q
+                    wide[pl.ds(first, steps, stride=group), :] = val[start : start + steps]
+    for peer in range(size):
+        rows = kxs * steps * group
+        part = wide[peer * rows : (peer + 1) * rows, :].astype(jnp.bfloat16)
+        held[peer] = part.reshape(kxs, steps, group, lanes)
+    source_of = lambda peer: held.at[peer]
+    place_of = lambda peer: out_ref.at[:, :, pl.ds(pl.multiple_of(peer * group, group), group)]
+    send_pieces("py", size, me, source_of, place_of(me), send_sem, recv_sem)
+    wait_pieces(size, me, source_of, place_of, send_sem, recv_sem)
+
+
+def back_column_kernel(size, steps, in_ref, table_ref, out_ref, held, wide, send_sem, recv_sem):
+    step = pl.program_id(0)
+    me = lax.axis_index("pz")
+    kxs = in_ref.shape[0]
+    _, nz, group, lanes = held.shape
+    zs = nz // size
+
+    @pl.when(step == 0)
+    def _():
+        greet("pz", size, me)
+
+    for kx in range(kxs):
+        val = dot(table_ref[...], in_ref[kx, 0])
+        for q in range(2):
+            wide[pl.ds(2 * kx + q, nz, stride=group), :] = val[q * nz : (q + 1) * nz]
+    held[step] = wide[...].astype(jnp.bfloat16).reshape(nz, group, lanes)
+
+    send_pieces(
+        "pz", size, me,
+        lambda peer: held.at[step, pl.ds(peer * zs, zs)],
+        out_ref.at[step, :, pl.ds(pl.multiple_of(me * group, group), group)],
+        send_sem, recv_sem,
+    )
+
+    @pl.when(step == steps - 1)
+    def _():
+        wait_pieces(
+            size, me,
+            lambda peer: held.at[:, pl.ds(peer * zs, zs)],
+            lambda peer: out_ref.at[:, :, pl.ds(pl.multiple_of(peer * group, group), group)],
+            send_sem, recv_sem,
+        )
+
+
+def point_kernel(in_ref, field_ref, table_ref, mix_ref, act_ref, sums_ref):
+    rows, zs, cs, nx = field_ref.shape
+
+    @pl.when(pl.program_id(0) == 0)
+    def _():
+        sums_ref[...] = jnp.zeros_like(sums_ref)
+
+    for z in range(zs):
+        spectral = lax.dot_general(
+            in_ref[0, z], table_ref[...], TN, preferred_element_type=jnp.float32
+        )
+        v = spectral + dot(mix_ref[...], field_ref[:, z].reshape(rows * cs, nx))
+        inner = math.sqrt(2.0 / math.pi) * (v + 0.044715 * (v * v * v))
+        act = 0.5 * v * (1.0 + jnp.tanh(inner))
+        act_ref[:, z] = act.astype(jnp.bfloat16).reshape(rows, cs, nx)
+        tall = act.reshape(-1, 8, nx)
+        sums_ref[0] += jnp.sum(tall, axis=0)
+        sums_ref[1] += jnp.sum(tall * tall, axis=0)
+
+
+def sum_kernel(py, pz, sums_ref, out_ref, mine, held, send_sem, recv_sem):
+    count = py * pz
+    me = lax.axis_index("py") * pz + lax.axis_index("pz")
+    peers = []
+    for step in range(1, count):
+        peer = lax.rem(me + step, count)
+        peers.append({"py": lax.div(peer, pz), "pz": lax.rem(peer, pz)})
+    barrier = pltpu.get_barrier_semaphore()
+    for peer in peers:
+        pl.semaphore_signal(barrier, inc=1, device_id=peer, device_id_type=MESH_ID)
+    for k in range(2):
+        total = jnp.sum(sums_ref[k], axis=0, keepdims=True)
+        total = sum(total[:, i : i + 128] for i in range(0, total.shape[1], 128))
+        mine[4 * k : 4 * k + 4, :] = jnp.broadcast_to(total, (4, 128))
+    pl.semaphore_wait(barrier, count - 1)
+    copies = []
+    for step, peer in enumerate(peers):
+        copy = pltpu.make_async_remote_copy(
+            src_ref=mine, dst_ref=held.at[step], send_sem=send_sem.at[step],
+            recv_sem=recv_sem.at[step], device_id=peer, device_id_type=MESH_ID,
+        )
+        copy.start()
+        copies.append(copy)
+    for copy in copies:
+        copy.wait()
+    total = mine[...] + jnp.sum(held[...], axis=0)
+    out_ref[...] = total
+
+
+def scale_kernel(entries, total_ref, act_ref, out_ref):
+    mean = jnp.sum(total_ref[0:1, :], keepdims=True)[:1, :1] / entries
+    square = jnp.sum(total_ref[4:5, :], keepdims=True)[:1, :1] / entries
+    scale = lax.rsqrt(square - mean * mean + 1e-05)
+    rows, zs, cs, nx = act_ref.shape
+    for z in range(zs):
+        v = act_ref[:, z].reshape(rows * cs, nx).astype(jnp.float32)
+        out_ref[:, z] = ((v - mean) * scale).astype(jnp.bfloat16).reshape(rows, cs, nx)
+
+
+def exchange_params(number):
+    return pltpu.CompilerParams(
+        collective_id=number, has_side_effects=True, vmem_limit_bytes=48 * 1024 * 1024
+    )
+
+
+ANY = pl.BlockSpec(memory_space=pl.ANY)
+WHOLE = pl.BlockSpec(memory_space=pltpu.VMEM)
+
+
+def on_device(py, pz, field, spectral_weights, bypass_weight):
+    ys, zs, cs, nx = field.shape
+    modes = spectral_weights.shape[2]
+    ny, nz = ys * py, zs * pz
+    steps, lanes, modes2 = ys // 2, 2 * cs, 2 * modes
+    kxs, kys, kzs = modes // pz, modes // pz, modes // py
+    aligned = lanes % 128 == 0 and zs % 16 == 0 and steps % 16 == 0 and kzs % 8 == 0
+    if not aligned or kxs % 4 or modes % 32:
+        return plain_layer(field, spectral_weights, bypass_weight)
+    row, column, plane, back_plane, back_column, inverse_row = np_tables(ny, nz, nx, modes)
+    bf16, f32 = jnp.bfloat16, jnp.float32
+    vmem, dma = pltpu.VMEM, pltpu.SemaphoreType.DMA
+    table = lambda t: pl.BlockSpec(t.shape, lambda i: (0,) * t.ndim)
+    field_block = pl.BlockSpec((2, zs, cs, nx), lambda i: (i, 0, 0, 0))
+
+    z_rows = pl.pallas_call(
+        functools.partial(row_kernel, pz, steps),
+        grid=(steps,),
+        out_shape=jax.ShapeDtypeStruct((steps, 2 * kxs, nz, lanes), bf16),
+        in_specs=[field_block, table(row)],
+        out_specs=ANY,
+        scratch_shapes=[
+            vmem((steps, modes2, zs, lanes), bf16), vmem((modes2 * zs, lanes), f32),
+            dma((pz,)), dma((pz,)),
+        ],
+        compiler_params=exchange_params(1),
+        name="row_modes",
+    )(field, row)
+
+    y_rows = pl.pallas_call(
+        functools.partial(column_kernel, py, steps),
+        grid=(steps,),
+        out_shape=jax.ShapeDtypeStruct((kxs, 2 * kzs, ny // 2, lanes), bf16),
+        in_specs=[pl.BlockSpec((1, 2 * kxs, nz, lanes), lambda i: (i, 0, 0, 0)), table(column)],
+        out_specs=ANY,
+        scratch_shapes=[
+            vmem((kxs, modes2, steps, lanes), bf16), vmem((kxs * modes2 * steps, lanes), f32),
+            dma((py,)), dma((py,)),
+        ],
+        compiler_params=exchange_params(2),
+        name="column_modes",
+    )(z_rows, column)
+
+    spectrum = pl.pallas_call(
+        plane_kernel,
+        grid=(kxs,),
+        out_shape=jax.ShapeDtypeStruct((kxs, kzs, modes2, cs), bf16),
+        in_specs=[pl.BlockSpec((1, 2 * kzs, ny // 2, lanes), lambda i: (i, 0, 0, 0)), table(plane)],
+        out_specs=pl.BlockSpec((1, kzs, modes2, cs), lambda i: (i, 0, 0, 0)),
+        name="plane_modes",
+    )(y_rows, plane)
+
+    moved = spectrum.reshape(kxs, kzs, modes, 2 * cs)
+    moved = lax.all_to_all(moved, "pz", split_axis=2, concat_axis=0, tiled=True)
+    moved = lax.all_to_all(moved, "py", split_axis=0, concat_axis=1, tiled=True)
+    moved = moved.transpose(0, 2, 1, 3)
+    real, imag = moved[..., :cs], moved[..., cs:]
+    lhs = jnp.stack([moved, jnp.concatenate([imag, real], -1)], axis=3)
+    sign = np.ones((2, 2 * cs), np.float32)
+    sign[0, cs:] = -1.0
+    lhs = lhs * jnp.asarray(sign, bf16)
+    stacked = spectral_weights.reshape(spectral_weights.shape[:3] + (2 * cs, cs))
+    mixed = jnp.einsum("abkqi,abkio->abkqo", lhs, stacked, preferred_element_type=f32).astype(bf16)
+    mixed = mixed.reshape(mixed.shape[:3] + (2 * cs,))
+    mixed = lax.all_to_all(mixed, "py", split_axis=2, concat_axis=0, tiled=True)
+    mixed = lax.all_to_all(mixed, "pz", split_axis=0, concat_axis=1, tiled=True)
+    mixed = mixed.transpose(0, 2, 1, 3).reshape(kxs, kzs, modes2, cs)
+
+    kz_rows = pl.pallas_call(
+        functools.partial(back_plane_kernel, py),
+        out_shape=jax.ShapeDtypeStruct((kxs, steps, modes2, lanes), bf16),
+        in_specs=[WHOLE, WHOLE],
+        out_specs=ANY,
+        scratch_shapes=[
+            vmem((py, kxs, steps, 2 * kzs, lanes), bf16),
+            vmem((py * kxs * steps * 2 * kzs, lanes), f32),
+            dma((py,)), dma((py,)),
+        ],
+        compiler_params=exchange_params(3),
+        name="plane_back",
+    )(mixed, back_plane)
+
+    kx_rows = pl.pallas_call(
+        functools.partial(back_column_kernel, pz, steps),
+        grid=(steps,),
+        out_shape=jax.ShapeDtypeStruct((steps, zs, modes2, lanes), bf16),
+        in_specs=[
+            pl.BlockSpec((kxs, 1, modes2, lanes), lambda i: (0, i, 0, 0)), table(back_column),
+        ],
+        out_specs=ANY,
+        scratch_shapes=[
+            vmem((steps, nz, 2 * kxs, lanes), bf16), vmem((nz * 2 * kxs, lanes), f32),
+            dma((pz,)), dma((pz,)),
+        ],
+        compiler_params=exchange_params(4),
+        name="column_back",
+    )(kz_rows, back_column)
+
+    flipped = bypass_weight.T
+    zero = jnp.zeros_like(flipped)
+    mix = jnp.concatenate(
+        [jnp.concatenate([flipped, zero], 1), jnp.concatenate([zero, flipped], 1)], 0
+    )
+    activated, sums = pl.pallas_call(
+        point_kernel,
+        grid=(steps,),
+        out_shape=[
+            jax.ShapeDtypeStruct(field.shape, bf16), jax.ShapeDtypeStruct((2, 8, nx), f32),
+        ],
+        in_specs=[
+            pl.BlockSpec((1, zs, modes2, lanes), lambda i: (i, 0, 0, 0)),
+            field_block, table(inverse_row), table(mix),
+        ],
+        out_specs=[field_block, pl.BlockSpec((2, 8, nx), lambda i: (0, 0, 0))],
+        name="points",
+    )(kx_rows, field, inverse_row, mix)
+
+    count = py * pz
+    total = pl.pallas_call(
+        functools.partial(sum_kernel, py, pz),
+        out_shape=jax.ShapeDtypeStruct((8, 128), f32),
+        in_specs=[WHOLE],
+        out_specs=WHOLE,
+        scratch_shapes=[
+            vmem((8, 128), f32), vmem((count - 1, 8, 128), f32), dma((count,)), dma((count,)),
+        ],
+        compiler_params=exchange_params(5),
+        name="totals",
+    )(sums)
+
+    return pl.pallas_call(
+        functools.partial(scale_kernel, float(ny * nz * cs * nx)),
+        grid=(steps,),
+        out_shape=jax.ShapeDtypeStruct(field.shape, bf16),
+        in_specs=[pl.BlockSpec((8, 128), lambda i: (0, 0)), field_block],
+        out_specs=field_block,
+        name="normalize",
+    )(total, activated)
+
+
 def solution(mesh):
     in_specs = (P("py", "pz", None, None), P("py", "pz", None, None, None, None), P())
     out_specs = P("py", "pz", None, None)
+    body = functools.partial(on_device, mesh.shape["py"], mesh.shape["pz"])
     return jax.shard_map(
-        on_device, mesh=mesh, in_specs=in_specs, out_specs=out_specs, check_vma=False
+        body, mesh=mesh, in_specs=in_specs, out_specs=out_specs, check_vma=False
     )

time: 530 us -> 281 us (0.53)
  Pallas kernels: 0 us -> 213 us
  waiting for transfers between devices: 193 us -> 4.64 us
  local copies, waits for them, and re-layouts: 124 us -> 8.36 us
  matrix products: 104 us -> 14 us
  blocking collectives: 61.6 us -> 31.9 us
  other arithmetic: 19.5 us -> 0.9 us
  starting transfers between devices: 18.7 us -> 4.8 us
    pallas_call x0 -> x8, Pallas kernels: none -> 213 us  [the longest x1 50.1 us: on_device(): pl.pallas_call(functools.partial(row_kernel, pz, steps), grid=(steps,), o...]
    all_to_all x3 -> x1, waiting for transfers between devices: 193 us -> 4.64 us  [on_device(): mixed = lax.all_to_all(mixed, 'pz', split_axis=0, concat_axis=1, tiled=True)]
    dot_general x11 -> x1, matrix products: 104 us -> 14 us  [on_device(): jnp.einsum('abkqi,abkio->abkqo', lhs, stacked, preferred_element_type=f32)]
    psum x1 -> x0, blocking collectives: 43.2 us -> none  [on_device(): lax.psum((jnp.sum(activated), jnp.sum(activated * activated)), ('py', 'pz'))]
    unnamed x10 -> x21, local copies, waits for them, and re-layouts: 46.5 us -> 5.16 us
    reshape x5, local copies, waits for them, and re-layouts: 40.6 us -> 2.06 us  [the longest x2 1.42 us: on_device(): moved = spectrum.reshape(kxs, kzs, modes, 2 * cs)]
    all_to_all x4 -> x5, local copies, waits for them, and re-layouts: 20.6 us -> 0.96 us  [the longest x2 0.86 us: on_device(): mixed = lax.all_to_all(mixed, 'py', split_axis=2, concat_axis=0, tiled=True)]
    convert_element_type x3 -> x0, other arithmetic: 18.5 us -> none  [the longest x1 18.5 us: on_device(): ((activated - field_mean) * lax.rsqrt(field_var + 1e-05)).astype(jnp.bflo...]
  transfers between devices with their start and end apart: 3 -> 1, of which waited for: 3 -> 1; matrix products, arithmetic and copies ran while one was open for 0% -> 0% of each run, Pallas kernels for 0% -> 0%
where the time goes in v1:
time: 281 us; the launch traced here: 277 us
  Pallas kernels  213 us (76%)
  blocking collectives  31.9 us (11%)
  matrix products  14 us (5%)
  local copies, waits for them, and re-layouts  8.36 us (3%)
  starting transfers between devices  4.8 us (2%)
  waiting for transfers between devices  4.64 us (2%)
    pallas_call x1, Pallas kernels, on_device(): pl.pallas_call(functools.partial(row_kernel, pz, steps), grid=(steps,), o...  50.1 us
    pallas_call x1, Pallas kernels, on_device(): pl.pallas_call(functools.partial(back_column_kernel, pz, steps), grid=(st...  49 us
    pallas_call x1, Pallas kernels, on_device(): pl.pallas_call(functools.partial(column_kernel, py, steps), grid=(steps,)...  30.3 us
    pallas_call x1, Pallas kernels, on_device(): pl.pallas_call(functools.partial(back_plane_kernel, py), out_shape=jax.Sh...  26.9 us
    pallas_call x1, Pallas kernels, on_device(): pl.pallas_call(point_kernel, grid=(steps,), out_shape=[jax.ShapeDtypeStru...  24.9 us
    pallas_call x1, Pallas kernels, on_device(): pl.pallas_call(functools.partial(scale_kernel, float(ny * nz * cs * nx)),...  19.4 us
    dot_general x1, matrix products, on_device(): jnp.einsum('abkqi,abkio->abkqo', lhs, stacked, preferred_element_type=f32)  14 us
    all_to_all x1, blocking collectives, on_device(): moved = lax.all_to_all(moved, 'py', split_axis=0, concat_axis=1, tiled=True)  11.5 us
  transfers between devices with their start and end apart: 1, of which 1 were waited for; matrix products, arithmetic and copies ran while one was open for 0% of the time, Pallas kernels for 0%

profile of v1, /device:TPU:12, one launch (start us, length us, event | category | flops | bytes accessed | tf_op | source)
XLA Modules:
  0.0 277.3 jit_solution(5348843956291250937)
XLA Ops:
  0.0 0.8 copy-done.3
  0.8 50.1 %row_modes.1.in_ref = bf16[16,8,128,128]{3,2,1,0:T(8,128)(2,1)S(1)} custom-call(bf16[32,16,64,256]{3,2,1,0:T(8,128)(2,1)} %field_ref.3, bf16[64,256]{1,0:T(8,128)(2,1)S(1)} %copy-done.3), custom_call_target="tpu_custom_call" | custom-call | tf_op jit(solution)/shard_map/row_modes/pallas_call | solution.py:420
  50.9 30.3 %column_modes.1.in_ref = bf16[4,16,64,128]{3,2,1,0:T(8,128)(2,1)S(1)} custom-call(bf16[16,8,128,128]{3,2,1,0:T(8,128)(2,1)S(1)} %row_modes.1.in_ref, bf16[64,256]{1,0:T(8,128)(2,1)S(1)} %copy-done.4), custom_call_target="tpu_custom_call" | custom-call | tf_op jit(solution)/shard_map/column_modes/pallas_call | solution.py:434
  81.2 1.0 copy-done.1
  82.1 3.8 %plane_modes.1 = bf16[4,8,64,64]{3,2,1,0:T(8,128)(2,1)} custom-call(bf16[4,16,64,128]{3,2,1,0:T(8,128)(2,1)} %copy-done.1, bf16[128,128]{1,0:T(8,128)(2,1)} %constant.18.clone.table_ref), custom_call_target="tpu_custom_call" | custom-call | tf_op jit(solution)/shard_map/plane_modes/pallas_call | solution.py:448
  86.0 1.3 reshape.13
  87.3 0.1 copy.26
  87.4 9.4 %all_to_all.72 = bf16[4,8,32,128]{3,1,0,2:T(8,128)(2,1)S(1)} all-to-all(bf16[4,8,32,128]{3,1,0,2:T(8,128)(2,1)S(1)} %copy.26), channel_id=1, replica_groups=mesh['py'=4,'pz'=8] {'pz'}, dimensions={2} | all-to-all | bytes 524288 | tf_op jit(solution)/shard_map/all_to_all | solution.py:458
  96.9 11.5 %all_to_all.73 = bf16[32,8,4,128]{3,1,2,0:T(8,128)(2,1)S(1)} all-to-all(bf16[32,8,4,128]{3,1,2,0:T(8,128)(2,1)S(1)} %bitcast.41), channel_id=1, replica_groups=mesh['py'=4,'pz'=8] {'py'}, dimensions={0} | all-to-all | bytes 524288 | tf_op jit(solution)/shard_map/all_to_all | solution.py:459
  108.4 0.1 fusion.4
  108.5 0.1 maximum_bitcast_fusion
  108.7 0.1 maximum_multiply_fusion
  108.8 0.0 copy-start.5
  108.8 14.0 %convolution_convert_fusion = bf16[8,4,32,2,64]{4,3,2,1,0:T(2,128)(2,1)S(1)} fusion(bf16[8,4,32,128,64]{4,3,2,1,0:T(8,128)(2,1)} %bitcast.36, bf16[8,4,32,2,128]{4,2,1,0,3:T(8,128)(2,1)S(1)} %maximum_multiply_fusion), kind=kOutput, calls=%fused_computation | convolution fusion | flops 33685504 | bytes 17563648 | tf_op jit(solution)/shard_map/abkqi,abkio->abkqo/dot_general | solution.py:467
  122.8 0.3 reshape.15
  123.1 0.1 copy.32
  123.2 11.0 %all_to_all.74 = bf16[8,4,32,128]{3,1,0,2:T(4,128)(2,1)S(1)} all-to-all(bf16[8,4,32,128]{3,1,0,2:T(4,128)(2,1)S(1)} %copy.32), channel_id=1, replica_groups=mesh['py'=4,'pz'=8] {'py'}, dimensions={2} | all-to-all | bytes 524288 | tf_op jit(solution)/shard_map/all_to_all | solution.py:469
  134.2 0.1 copy.45
  134.3 0.8 copy.34
  135.0 4.8 %all-to-all-start.3 = ((bf16[32,4,8,128]{3,2,1,0:T(8,128)(2,1)}), bf16[32,4,8,128]{3,2,1,0:T(8,128)(2,1)S(1)}, u32[]{:S(2)}, u32[]{:S(2)}) async-start(bf16[32,4,8,128]{3,2,1,0:T(8,128)(2,1)} %bitcast.14), calls=%async_computation.3 | async-start | bytes 524288 | tf_op jit(solution)/shard_map/all_to_all | solution.py:470
  139.8 0.1 copy.37
  139.9 0.7 fusion.3.mix_ref
  140.6 4.6 %all-to-all-done.3 = bf16[32,4,8,128]{3,2,1,0:T(8,128)(2,1)S(1)} async-done(((bf16[32,4,8,128]{3,2,1,0:T(8,128)(2,1)}), bf16[32,4,8,128]{3,2,1,0:T(8,128)(2,1)S(1)}, u32[]{:S(2)}, u32[]{:S(2)}) %all-to-all-start.3) | async-done | bytes 262176 | tf_op jit(solution)/shard_map/all_to_all | solution.py:470
  145.3 0.2 reshape.16.in_ref
  145.6 26.9 %plane_back.1.in_ref = bf16[4,16,64,128]{3,2,1,0:T(8,128)(2,1)S(1)} custom-call(bf16[4,8,64,64]{3,2,1,0:T(8,128)(2,1)S(1)} %reshape.16.in_ref, bf16[128,128]{1,0:T(8,128)(2,1)S(1)} %copy-done.5), custom_call_target="tpu_custom_call" | custom-call | tf_op jit(solution)/shard_map/plane_back/pallas_call | solution.py:473
  172.5 49.0 %column_back.1.in_ref = bf16[16,16,64,128]{3,2,1,0:T(8,128)(2,1)S(1)} custom-call(bf16[4,16,64,128]{3,2,1,0:T(8,128)(2,1)S(1)} %plane_back.1.in_ref, bf16[256,64]{1,0:T(8,128)(2,1)S(1)} %copy-done.2), custom_call_target="tpu_custom_call" | custom-call | tf_op jit(solution)/shard_map/column_back/pallas_call | solution.py:487
  221.6 2.0 copy-done
  223.6 24.9 %points.1 = (bf16[32,16,64,256]{3,2,1,0:T(8,128)(2,1)}, f32[2,8,256]{2,1,0:T(8,128)}) custom-call(bf16[16,16,64,128]{3,2,1,0:T(8,128)(2,1)} %copy-done, bf16[32,16,64,256]{3,2,1,0:T(8,128)(2,1)} %field_ref.3, bf16[64,256]{1,0:T(8,128)(2,1)} %constant.22.clone.table_ref, bf16[128,128]{1,0:T(8,128)(2,1)} %fusion.3.mix_ref), custom_call_target="tpu_custom_call" | custom-call | tf_op jit(solution)/shard_map/points/pallas_call | solution.py:508
  248.5 0.7 copy-done.7
  249.2 8.1 %totals.1.total_ref = f32[8,128]{1,0:T(8,128)S(1)} custom-call(f32[2,8,256]{2,1,0:T(8,128)S(1)} %copy-done.7), custom_call_target="tpu_custom_call" | custom-call | tf_op jit(solution)/shard_map/totals/pallas_call | solution.py:523
  257.3 0.6 copy-done.6
  257.9 19.4 %normalize.1 = bf16[32,16,64,256]{3,2,1,0:T(8,128)(2,1)} custom-call(f32[8,128]{1,0:T(8,128)} %copy-done.6, bf16[32,16,64,256]{3,2,1,0:T(8,128)(2,1)} %get-tuple-element.8.act_ref), custom_call_target="tpu_custom_call" | custom-call | tf_op jit(solution)/shard_map/normalize/pallas_call | solution.py:535
  (18 shorter events, 0.2 us)
Async XLA Ops:
  0.0 108.7 %copy-start.9 = (bf16[2,128]{1,0:T(2,128)(2,1)S(1)}, bf16[2,128]{1,0:T(2,128)(2,1)}, u32[]{:S(2)}) copy-start(bf16[2,128]{1,0:T(2,128)(2,1)} %constant.19.clone) | copy-start | bytes 1540
  0.0 0.8 copy-start.3
  0.8 50.1 %copy-start.4 = (bf16[64,256]{1,0:T(8,128)(2,1)S(1)}, bf16[64,256]{1,0:T(8,128)(2,1)}, u32[]{:S(2)}) copy-start(bf16[64,256]{1,0:T(8,128)(2,1)} %constant.17.clone.table_ref) | copy-start | bytes 98308
  81.2 1.0 copy-start.1
  108.8 31.1 %copy-start.8 = (bf16[64,64]{1,0:T(8,128)(2,1)S(1)}, bf16[64,64]{1,0:T(8,128)(2,1)}, u32[]{:S(2)}) copy-start(bf16[64,64]{1,0:T(8,128)(2,1)} %param.12) | copy-start | bytes 24580
  108.8 36.8 %copy-start.5 = (bf16[128,128]{1,0:T(8,128)(2,1)S(1)}, bf16[128,128]{1,0:T(8,128)(2,1)}, u32[]{:S(2)}) copy-start(bf16[128,128]{1,0:T(8,128)(2,1)} %constant.20.clone.table_ref) | copy-start | bytes 98308
  108.8 63.7 %copy-start.2 = (bf16[256,64]{1,0:T(8,128)(2,1)S(1)}, bf16[256,64]{1,0:T(8,128)(2,1)}, u32[]{:S(2)}) copy-start(bf16[256,64]{1,0:T(8,128)(2,1)} %constant.21.clone.table_ref) | copy-start | bytes 98308
  135.0 10.2 %all-to-all-start.3 = ((bf16[32,4,8,128]{3,2,1,0:T(8,128)(2,1)}), bf16[32,4,8,128]{3,2,1,0:T(8,128)(2,1)S(1)}, u32[]{:S(2)}, u32[]{:S(2)}) async-start(bf16[32,4,8,128]{3,2,1,0:T(8,128)(2,1)} %bitcast.14), calls=%async_computation.3 | async-start | bytes 524288 | tf_op jit(solution)/shard_map/all_to_all | solution.py:470
  221.5 2.0 copy-start
  248.5 0.7 copy-start.7
  257.3 0.6 copy-start.6
